TPU v7x, 32 devices: a whole 2x2x4 slice. The times are simulated.
32 devices in a mesh: limb: 4 (over z), coef: 8 (over y, x, core).
Axes of the slice: x: 2, y: 2, z: 4, core: 2. Of those that a mesh axis runs over, the one named last changes fastest.
Arguments:
- cipher_zero: float32 [24, 32, 65536], P(None, 'limb', 'coef'), may hold values from -6 to 6
- cipher_one: float32 [24, 32, 65536], P(None, 'limb', 'coef'), may hold values from -6 to 6
- key_main: bfloat16 [24, 2, 2, 32, 65536], P(None, None, None, 'limb', 'coef'), may hold values from -5 to 5
- key_special: bfloat16 [24, 2, 2, 16, 65536], P(None, None, None, 'limb', 'coef'), may hold values from -5 to 5
- lift_main: float32 [32, 32], replicated, may hold values from -1.5 to 1.5
- lift_special: float32 [32, 16], replicated, may hold values from -1.5 to 1.5
- lower_table: float32 [16, 32], replicated, may hold values from -1.5 to 1.5
- inverse_scale: float32 [32], P('limb'), may hold values from 0.5 to 1.5
- inverse_main: float32 [32, 256, 256], P('limb', 'coef'), may hold values from 0.5 to 1.5
- inverse_special: float32 [16, 256, 256], P('limb', 'coef'), may hold values from 0.5 to 1.5
- forward_main: float32 [32, 256, 256], P('limb', 'coef'), may hold values from 0.5 to 1.5
- forward_special: float32 [16, 256, 256], P('limb', 'coef'), may hold values from 0.5 to 1.5
- inverse_rows: float32 [256, 256], replicated, may hold values from -0.375 to 0.375
- inverse_columns: float32 [256, 256], replicated, may hold values from -0.375 to 0.375
- forward_rows: float32 [256, 256], replicated, may hold values from -0.375 to 0.375
- forward_columns: float32 [256, 256], replicated, may hold values from -0.375 to 0.375
Outputs:
- switched_zero: float32 [24, 32, 65536], P(None, 'limb', 'coef')
- switched_one: float32 [24, 32, 65536], P(None, 'limb', 'coef')
All inputs are finite; a program needn't handle non-finite values.
Results may differ from a plain program's by a relative error of at most 0.0003.
Values sent between devices are 32-bit elements; how exact they have to be, the bound alone decides.
No kernel may reach another device: no remote copies, remote signals or barrier semaphores. Data moves between devices by JAX's collectives and lax.ppermute only.
A program may use at most 192 MiB of HBM per device.

v0:
```python
import jax
import jax.numpy as jnp
from jax import lax
from jax.sharding import PartitionSpec as P

K = 16
ROWS = 256
COLS = 256
HIGHEST = lax.Precision.HIGHEST


def columns_section(values, twiddle, inverse_columns):
    partial_value = (
        jnp.einsum("...rc,ck->...rk", values, inverse_columns, precision=HIGHEST) * twiddle
    )
    flattened = partial_value.reshape((-1,) + partial_value.shape[-2:])
    return lax.all_to_all(flattened, "coef", split_axis=2, concat_axis=1, tiled=True)


def to_coefficients(values, twiddle, inverse_rows, inverse_columns):
    leading = values.shape[:-2]
    arrived = columns_section(values, twiddle, inverse_columns)
    output = jnp.einsum("brk,rj->bkj", arrived, inverse_rows, precision=HIGHEST)
    return output.reshape(leading + output.shape[-2:])


def to_values(coeffs, twiddle, forward_rows, forward_columns):
    leading = coeffs.shape[:-2]
    partial_value = jnp.einsum("...cr,rk->...ck", coeffs, forward_rows, precision=HIGHEST) * twiddle
    flattened = partial_value.reshape((-1,) + partial_value.shape[-2:])
    arrived = lax.all_to_all(flattened, "coef", split_axis=2, concat_axis=1, tiled=True)
    output = jnp.einsum("bck,cm->bkm", arrived, forward_columns, precision=HIGHEST)
    return output.reshape(leading + output.shape[-2:])


def on_device(
    cipher_zero,
    cipher_one,
    key_main,
    key_special,
    lift_main,
    lift_special,
    lower_table,
    inverse_scale,
    inverse_main,
    inverse_special,
    forward_main,
    forward_special,
    inverse_rows,
    inverse_columns,
    forward_rows,
    forward_columns,
):
    ciphers, local_main, positions = cipher_one.shape
    local_special = key_special.shape[3]
    digits = key_main.shape[1]
    rows_here = inverse_main.shape[1]
    cols_here = forward_main.shape[1]
    total_main = lift_main.shape[0]
    limb_index = lax.axis_index("limb")
    owner = (jnp.arange(total_main) // K)[None, :] == jnp.arange(digits)[:, None]
    digit_mask = owner.astype(lift_main.dtype)
    masked_main = digit_mask[:, :, None] * lift_main[None]
    masked_special = digit_mask[:, :, None] * lift_special[None]
    twiddle_both = jnp.concatenate([forward_main, forward_special], axis=0)
    shaped = cipher_one.reshape(ciphers, local_main, rows_here, COLS)
    coeffs = to_coefficients(shaped, inverse_main, inverse_rows, inverse_columns).reshape(
        ciphers, local_main, positions
    )
    own_main = lax.dynamic_slice_in_dim(masked_main, limb_index * local_main, local_main, 2)
    own_special = lax.dynamic_slice_in_dim(
        masked_special, limb_index * local_special, local_special, 2
    )
    portion = lax.all_gather(coeffs, "limb", axis=1, tiled=True)
    lifted_main = jnp.einsum("bsn,dst->bdtn", portion, own_main, precision=HIGHEST)
    lifted_sp = jnp.einsum("bsn,dst->bdtn", portion, own_special, precision=HIGHEST)
    joined = jnp.concatenate([lifted_main, lifted_sp], axis=2)
    joined = joined.reshape(ciphers, digits, local_main + local_special, cols_here, ROWS)
    values_all = to_values(joined, twiddle_both, forward_rows, forward_columns)
    values_all = values_all.reshape(ciphers, digits, local_main + local_special, positions)
    values_main = values_all[:, :, :local_main]
    values_sp = values_all[:, :, local_main:]
    summed_main = jnp.sum(values_main[:, :, None] * key_main.astype(jnp.float32), axis=1)
    summed_sp = jnp.sum(values_sp[:, :, None] * key_special.astype(jnp.float32), axis=1)
    shaped_sp = summed_sp.reshape(ciphers, 2, local_special, rows_here, COLS)
    special = to_coefficients(shaped_sp, inverse_special, inverse_rows, inverse_columns)
    special = special.reshape(ciphers, 2, local_special, positions)
    own_lower = lax.dynamic_slice_in_dim(lower_table, limb_index * local_main, local_main, 1)
    lowered = jnp.einsum(
        "bsjn,jt->bstn",
        lax.all_gather(special, "limb", axis=2, tiled=True),
        own_lower,
        precision=HIGHEST,
    )
    lowered = to_values(
        lowered.reshape(ciphers, 2, local_main, cols_here, ROWS),
        forward_main,
        forward_rows,
        forward_columns,
    )
    lowered = lowered.reshape(ciphers, 2, local_main, positions)
    result = inverse_scale[:, None] * (summed_main - lowered)
    return (cipher_zero + result[:, 0], result[:, 1])


def solution(mesh):
    placed = (
        P(None, "limb", "coef"),
        P(None, "limb", "coef"),
        P(None, None, None, "limb", "coef"),
        P(None, None, None, "limb", "coef"),
        P(),
        P(),
        P(),
        P("limb"),
        P("limb", "coef", None),
        P("limb", "coef", None),
        P("limb", "coef", None),
        P("limb", "coef", None),
        P(),
        P(),
        P(),
        P(),
    )
    return jax.shard_map(
        on_device,
        mesh=mesh,
        in_specs=placed,
        out_specs=(P(None, "limb", "coef"), P(None, "limb", "coef")),
        check_vma=False,
    )
```

profile of v0, /device:TPU:0, one launch (start us, length us, event | category | flops | bytes accessed | tf_op | source)
XLA Modules:
  0.0 1902.5 jit_solution(8218457899947715766)
XLA Ops:
  7.2 10.8 broadcast_multiply_fusion.3
  18.0 9.6 copy.48
  27.6 99.7 %all_to_all.72 = f32[192,32,256]{0,1,2:T(8,128)S(1)} all-to-all(f32[192,32,256]{0,1,2:T(8,128)} %copy.48), channel_id=1, replica_groups=mesh['limb'=4,'coef'=8] {'coef'}, dimensions={2} | all-to-all | bytes 12582912 | tf_op jit(solution)/shard_map/all_to_all | solution.py:17
  135.2 9.7 copy.51
  162.7 423.1 %all-gather.3.cloned.1.call-done = f32[24,32,8192]{2,1,0:T(8,128)} async-done(((f32[24,8,8192]{2,1,0:T(8,128)}), f32[24,32,8192]{2,1,0:T(8,128)}) %all-gather.3.cloned.1.call-update) | async-done | bytes 25165840 | tf_op jit(solution)/shard_map/all_gather | solution.py:74
  585.8 16.9 fusion.13
  602.7 15.7 fusion.10
  618.5 14.2 pad_maximum_fusion
  632.7 21.5 %reshape.87 = f32[24,2,12,32,256]{4,3,2,0,1:T(8,128)} reshape(f32[24,2,12,8192]{3,2,0,1:T(8,128)} %pad_maximum_fusion) | data formatting | bytes 37748736 | tf_op jit(solution)/shard_map/reshape | solution.py:78
  654.2 20.6 %broadcast_multiply_fusion = f32[24,2,12,32,256]{4,3,2,1,0:T(8,128)} fusion(f32[12,32,256]{2,1,0:T(8,128)S(1)} %pad_maximum_fusion.1, f32[24,2,12,32,256]{4,3,2,0,1:T(8,128)} %reshape.87, f32[256,256]{1,0:T(8,128)S(1)} %copy-done), kind=kOutput, calls=%fused_computation.16 | convolution fusion | flops 14500233216 | bytes 38404096 | tf_op jit(solution)/shard_map/...cr,rk->...ck/dot_general | solution.py:29
  674.8 23.4 %copy.54 = f32[576,32,256]{0,1,2:T(8,128)} copy(f32[576,32,256]{2,1,0:T(8,128)} %bitcast.95) | data formatting | bytes 37748736 | tf_op jit(solution)/shard_map/reshape | solution.py:30
  698.2 233.5 %all_to_all.73 = f32[576,32,256]{0,1,2:T(8,128)S(1)} all-to-all(f32[576,32,256]{0,1,2:T(8,128)} %copy.54), channel_id=1, replica_groups=mesh['limb'=4,'coef'=8] {'coef'}, dimensions={2} | all-to-all | bytes 37748736 | tf_op jit(solution)/shard_map/all_to_all | solution.py:31
  931.8 14.1 copy.56
  945.9 21.5 %copy.57 = f32[576,256,32]{1,2,0:T(8,128)} copy(f32[576,256,32]{0,2,1:T(8,128)} %bitcast.97) | data formatting | bytes 37748736 | tf_op jit(solution)/shard_map/all_to_all | solution.py:31
  967.4 20.2 %fusion.31 = f32[576,32,256]{2,1,0:T(8,128)} fusion(f32[576,256,32]{1,2,0:T(8,128)} %copy.57, f32[256,256]{1,0:T(8,128)S(1)} %copy-done.2), kind=kOutput, calls=%fused_computation.32 | convolution fusion | flops 14495514624 | bytes 38010880 | tf_op jit(solution)/shard_map/bck,cm->bkm/dot_general | solution.py:32
  987.6 20.6 %reshape_reshape.13 = f32[24,2,12,8192]{3,2,1,0:T(8,128)} reshape(f32[576,32,256]{2,1,0:T(8,128)} %fusion.31) | data formatting | bytes 37748736 | tf_op jit(solution)/shard_map/reshape;reshape | solution.py:80
  1013.7 11.3 multiply_reduce_fusion.1
  1042.6 9.6 copy.59
  1052.2 97.8 %all_to_all.74 = f32[192,32,256]{0,1,2:T(8,128)S(1)} all-to-all(f32[192,32,256]{0,1,2:T(8,128)} %copy.59), channel_id=1, replica_groups=mesh['limb'=4,'coef'=8] {'coef'}, dimensions={2} | all-to-all | bytes 12582912 | tf_op jit(solution)/shard_map/all_to_all | solution.py:17
  1157.9 9.7 copy.62
  1194.3 421.7 %all-gather.5.cloned.1.call-done = f32[24,2,16,8192]{3,0,1,2:T(8,128)} async-done(((f32[24,2,4,8192]{3,0,1,2:T(8,128)}), f32[24,2,16,8192]{3,0,1,2:T(8,128)}) %all-gather.5.cloned.1.call-update) | async-done | bytes 25165840 | tf_op jit(solution)/shard_map/all_gather | solution.py:91
  1615.9 34.7 %fusion.4 = f32[8,24,2,8192]{3,0,2,1:T(8,128)S(1)} fusion(f32[24,2,16,8192]{3,0,1,2:T(8,128)} %all-gather.5.cloned.1.call-done, f32[16,32]{1,0:T(8,128)S(1)} %copy-done.12, s32[]{:T(128)S(6)} %select_n.19), kind=kOutput, calls=%fused_computation.5 | convolution fusion | flops 603979776 | bytes 37750788 | tf_op jit(solution)/shard_map/bsjn,jt->bstn/dot_general | solution.py:89
  1650.7 13.7 broadcast_multiply_fusion.1
  1664.4 12.9 copy.66
  1682.6 10.4 slice.16
  1693.1 15.5 multiply_reduce_fusion
  1708.6 113.0 %all-to-all-done.3 = f32[384,32,256]{0,1,2:T(8,128)} async-done(((f32[384,32,256]{0,1,2:T(8,128)}), f32[384,32,256]{0,1,2:T(8,128)}, u32[]{:S(2)}, u32[]{:S(2)}) %all-to-all-start.3) | async-done | bytes 12582944 | tf_op jit(solution)/shard_map/all_to_all | solution.py:31
  1821.6 16.1 copy.68
  1837.8 12.9 copy.77
  1850.7 14.9 fusion.29
  1865.6 14.0 reshape_reshape.15
  1879.6 9.3 subtract_multiply_fusion
  (56 shorter events, 95.3 us)
Async XLA Ops:
  7.2 647.0 %copy-start = (f32[256,256]{1,0:T(8,128)S(1)}, f32[256,256]{1,0:T(8,128)}, u32[]{:S(2)}) copy-start(f32[256,256]{1,0:T(8,128)} %param.30) | copy-start | bytes 786436
  7.2 578.6 %all-gather.3.cloned.1.call-start = ((), (), s32[]{:S(2)}) async-start(), calls=%async_computation.4 | async-start | bytes 31457280 | tf_op jit(solution)/shard_map/all_gather | solution.py:74
  127.3 17.7 copy-start.7
  153.8 7.5 copy-start.11
  153.8 8.2 copy-start.4
  153.8 8.2 copy-start.10
  161.0 1454.9 %all-gather.5.cloned.1.call-start = ((), (), s32[]{:S(2)}) async-start(), calls=%async_computation.5 | async-start | bytes 31457280 | tf_op jit(solution)/shard_map/all_gather | solution.py:91
  585.8 17.0 copy-start.1
  945.9 21.5 %copy-start.2 = (f32[256,256]{1,0:T(8,128)S(1)}, f32[256,256]{1,0:T(8,128)}, u32[]{:S(2)}) copy-start(f32[256,256]{1,0:T(8,128)} %param.31) | copy-start | bytes 786436
  1013.7 19.9 %copy-start.9 = (f32[4,32,256]{2,1,0:T(8,128)S(1)}, f32[4,32,256]{2,1,0:T(8,128)}, u32[]{:S(2)}) copy-start(f32[4,32,256]{2,1,0:T(8,128)} %param.25) | copy-start | bytes 393220
  1025.0 8.5 copy-start.6
  1149.9 17.7 copy-start.8
  1185.1 430.8 %copy-start.12 = (f32[16,32]{1,0:T(8,128)S(1)}, f32[16,32]{1,0:T(8,128)}, u32[]{:S(2)}) copy-start(f32[16,32]{1,0:T(8,128)} %param.22) | copy-start | bytes 6148
  1194.2 456.4 %copy-start.5 = (f32[8,32,256]{2,1,0:T(8,128)S(1)}, f32[8,32,256]{2,1,0:T(8,128)}, u32[]{:S(2)}) copy-start(f32[8,32,256]{2,1,0:T(8,128)} %param.26) | copy-start | bytes 786436
  1677.2 144.4 %all-to-all-start.3 = ((f32[384,32,256]{0,1,2:T(8,128)}), f32[384,32,256]{0,1,2:T(8,128)}, u32[]{:S(2)}, u32[]{:S(2)}) async-start(f32[384,32,256]{0,1,2:T(8,128)} %copy.66), calls=%async_computation.3 | async-start | bytes 25165824 | tf_op jit(solution)/shard_map/all_to_all | solution.py:31
  1837.8 12.9 copy-start.3
  1865.6 14.0 copy-start.13
  1865.6 26.4 %slice-start = ((s8[6291456]{0:T(1024)(128)(4,1)}), s8[2097152]{0:T(1024)(128)(4,1)S(1)}, s32[]{:S(2)}) async-start(s8[6291456]{0:T(1024)(128)(4,1)} %bitcast.108), calls=%async_computation.6 | async-start | bytes 4194304
  1879.6 12.4 slice-start.1
Sparse Core Ops, SparseCore 0:
  161.1 424.5 all-gather.2
  1194.4 421.5 all-gather.4
where the time goes:
time: 1910 us; the launch traced here: 1900 us
  waiting for transfers between devices  958 us (50%)
  blocking collectives  431 us (23%)
  local copies, waits for them, and re-layouts  265 us (14%)
  matrix products  174 us (9%)
  other arithmetic  54.3 us (3%)
    all_gather x1, waiting for transfers between devices, on_device(): portion = lax.all_gather(coeffs, 'limb', axis=1, tiled=True)  423 us
    all_gather x1, waiting for transfers between devices, on_device(): lax.all_gather(special, 'limb', axis=2, tiled=True)  422 us
    all_to_all x1, blocking collectives, to_values(): lax.all_to_all(flattened, 'coef', split_axis=2, concat_axis=1, tiled=True)  234 us
    all_to_all x2, blocking collectives, columns_section(): lax.all_to_all(flattened, 'coef', split_axis=2, concat_axis=1, tiled=True)  197 us
    all_to_all x1, waiting for transfers between devices, to_values(): lax.all_to_all(flattened, 'coef', split_axis=2, concat_axis=1, tiled=True)  113 us
    all_to_all x4, local copies, waits for them, and re-layouts, to_values(): lax.all_to_all(flattened, 'coef', split_axis=2, concat_axis=1, tiled=True)  64.7 us
  transfers between devices with their start and end apart: 3, of which 3 were waited for; matrix products, arithmetic and copies ran while one was open for 1% of the time, Pallas kernels for 0%

commit v1 on v0

--- a/solution.py
+++ b/solution.py
@@ -88,7 +88,7 @@
     own_lower = lax.dynamic_slice_in_dim(lower_table, limb_index * local_main, local_main, 1)
     lowered = jnp.einsum(
         "bsjn,jt->bstn",
-        lax.all_gather(special, "limb", axis=2, tiled=True),
+        jnp.concatenate(lax.all_gather(special, "limb"), axis=2),
         own_lower,
         precision=HIGHEST,
     )

time: 1910 us -> 1950 us (1.021)
  local copies, waits for them, and re-layouts: 265 us -> 324 us
    reshape x0 -> x2, local copies, waits for them, and re-layouts: none -> 58.8 us  [on_device(): jnp.concatenate(lax.all_gather(special, 'limb'), axis=2)]
where the time goes in v1:
time: 1950 us; the launch traced here: 1940 us
  waiting for transfers between devices  958 us (49%)
  blocking collectives  431 us (22%)
  local copies, waits for them, and re-layouts  324 us (17%)
  matrix products  157 us (8%)
  other arithmetic  54.3 us (3%)
    all_gather x1, waiting for transfers between devices, on_device(): portion = lax.all_gather(coeffs, 'limb', axis=1, tiled=True)  423 us
    all_gather x1, waiting for transfers between devices, on_device(): lax.all_gather(special, 'limb')  422 us
    all_to_all x1, blocking collectives, to_values(): lax.all_to_all(flattened, 'coef', split_axis=2, concat_axis=1, tiled=True)  234 us
    all_to_all x2, blocking collectives, columns_section(): lax.all_to_all(flattened, 'coef', split_axis=2, concat_axis=1, tiled=True)  197 us
    all_to_all x1, waiting for transfers between devices, to_values(): lax.all_to_all(flattened, 'coef', split_axis=2, concat_axis=1, tiled=True)  113 us
    all_to_all x4, local copies, waits for them, and re-layouts, to_values(): lax.all_to_all(flattened, 'coef', split_axis=2, concat_axis=1, tiled=True)  64.7 us
    reshape x2, local copies, waits for them, and re-layouts, on_device(): jnp.concatenate(lax.all_gather(special, 'limb'), axis=2)  58.8 us
  transfers between devices with their start and end apart: 3, of which 3 were waited for; matrix products, arithmetic and copies ran while one was open for 1% of the time, Pallas kernels for 0%

profile of v1, /device:TPU:0, one launch (start us, length us, event | category | flops | bytes accessed | tf_op | source)
XLA Modules:
  0.0 1944.1 jit_solution(12884193095064419766)
XLA Ops:
  7.2 10.8 broadcast_multiply_fusion.3
  18.0 9.6 copy.50
  27.6 99.4 %all_to_all.72 = f32[192,32,256]{0,1,2:T(8,128)S(1)} all-to-all(f32[192,32,256]{0,1,2:T(8,128)} %copy.50), channel_id=1, replica_groups=mesh['limb'=4,'coef'=8] {'coef'}, dimensions={2} | all-to-all | bytes 12582912 | tf_op jit(solution)/shard_map/all_to_all | solution.py:17
  134.9 9.7 copy.53
  162.3 423.1 %all-gather.3.cloned.1.call-done = f32[24,32,8192]{2,1,0:T(8,128)} async-done(((f32[24,8,8192]{2,1,0:T(8,128)}), f32[24,32,8192]{2,1,0:T(8,128)}) %all-gather.3.cloned.1.call-update) | async-done | bytes 25165840 | tf_op jit(solution)/shard_map/all_gather | solution.py:74
  585.4 16.9 fusion.11
  602.4 15.7 fusion.8
  618.1 14.2 pad_maximum_fusion
  632.3 21.5 %reshape.95 = f32[24,2,12,32,256]{4,3,2,0,1:T(8,128)} reshape(f32[24,2,12,8192]{3,2,0,1:T(8,128)} %pad_maximum_fusion) | data formatting | bytes 37748736 | tf_op jit(solution)/shard_map/reshape | solution.py:78
  653.8 20.6 %broadcast_multiply_fusion = f32[24,2,12,32,256]{4,3,2,1,0:T(8,128)} fusion(f32[12,32,256]{2,1,0:T(8,128)S(1)} %pad_maximum_fusion.1, f32[24,2,12,32,256]{4,3,2,0,1:T(8,128)} %reshape.95, f32[256,256]{1,0:T(8,128)S(1)} %copy-done), kind=kOutput, calls=%fused_computation.14 | convolution fusion | flops 14500233216 | bytes 38404096 | tf_op jit(solution)/shard_map/...cr,rk->...ck/dot_general | solution.py:29
  674.5 23.4 %copy.56 = f32[576,32,256]{0,1,2:T(8,128)} copy(f32[576,32,256]{2,1,0:T(8,128)} %bitcast.98) | data formatting | bytes 37748736 | tf_op jit(solution)/shard_map/reshape | solution.py:30
  697.9 233.6 %all_to_all.73 = f32[576,32,256]{0,1,2:T(8,128)S(1)} all-to-all(f32[576,32,256]{0,1,2:T(8,128)} %copy.56), channel_id=1, replica_groups=mesh['limb'=4,'coef'=8] {'coef'}, dimensions={2} | all-to-all | bytes 37748736 | tf_op jit(solution)/shard_map/all_to_all | solution.py:31
  931.5 14.1 copy.58
  945.6 21.5 %copy.59 = f32[576,256,32]{1,2,0:T(8,128)} copy(f32[576,256,32]{0,2,1:T(8,128)} %bitcast.100) | data formatting | bytes 37748736 | tf_op jit(solution)/shard_map/all_to_all | solution.py:31
  967.1 20.2 %fusion.29 = f32[576,32,256]{2,1,0:T(8,128)} fusion(f32[576,256,32]{1,2,0:T(8,128)} %copy.59, f32[256,256]{1,0:T(8,128)S(1)} %copy-done.2), kind=kOutput, calls=%fused_computation.30 | convolution fusion | flops 14495514624 | bytes 38010880 | tf_op jit(solution)/shard_map/bck,cm->bkm/dot_general | solution.py:32
  987.3 20.6 %reshape_reshape.10 = f32[24,2,12,8192]{3,2,1,0:T(8,128)} reshape(f32[576,32,256]{2,1,0:T(8,128)} %fusion.29) | data formatting | bytes 37748736 | tf_op jit(solution)/shard_map/reshape;reshape | solution.py:80
  1013.4 11.3 multiply_reduce_fusion.1
  1051.9 97.8 %all_to_all.74 = f32[192,32,256]{0,1,2:T(8,128)S(1)} all-to-all(f32[192,32,256]{0,1,2:T(8,128)} %copy.61), channel_id=1, replica_groups=mesh['limb'=4,'coef'=8] {'coef'}, dimensions={2} | all-to-all | bytes 12582912 | tf_op jit(solution)/shard_map/all_to_all | solution.py:17
  1157.6 9.7 copy.64
  1193.9 421.7 %all-gather.5.cloned.1.call-done = f32[4,24,2,4,8192]{4,1,3,2,0:T(8,128)} async-done(((f32[1,24,2,4,8192]{4,1,3,2,0:T(8,128)}), f32[4,24,2,4,8192]{4,1,3,2,0:T(8,128)}) %all-gather.5.cloned.1.call-update) | async-done | bytes 25165840 | tf_op jit(solution)/shard_map/all_gather | solution.py:91
  1615.6 30.0 %copy.66 = f32[24,2,4,4,8192]{4,3,2,1,0:T(4,128)} copy(f32[24,2,4,4,8192]{4,0,3,1,2:T(8,128)} %bitcast.108) | data formatting | bytes 50331648 | tf_op jit(solution)/shard_map/reshape | solution.py:91
  1645.6 28.8 %reshape.83 = f32[24,2,16,8192]{3,2,1,0:T(8,128)} reshape(f32[24,2,4,4,8192]{4,3,2,1,0:T(4,128)} %copy.66) | data formatting | bytes 50331648 | tf_op jit(solution)/shard_map/reshape | solution.py:91
  1674.5 17.3 fusion.35
  1691.7 14.1 broadcast_multiply_fusion.1
  1705.8 12.9 copy.68
  1724.3 10.4 slice.16
  1734.7 15.5 multiply_reduce_fusion
  1750.2 113.0 %all-to-all-done.3 = f32[384,32,256]{0,1,2:T(8,128)} async-done(((f32[384,32,256]{0,1,2:T(8,128)}), f32[384,32,256]{0,1,2:T(8,128)}, u32[]{:S(2)}, u32[]{:S(2)}) %all-to-all-start.3) | async-done | bytes 12582944 | tf_op jit(solution)/shard_map/all_to_all | solution.py:31
  1863.2 16.1 copy.70
  1879.4 12.9 copy.79
  1892.3 14.9 fusion.27
  1907.3 14.0 reshape_reshape.11
  (58 shorter events, 114.3 us)
Async XLA Ops:
  7.2 646.7 %copy-start = (f32[256,256]{1,0:T(8,128)S(1)}, f32[256,256]{1,0:T(8,128)}, u32[]{:S(2)}) copy-start(f32[256,256]{1,0:T(8,128)} %param.30) | copy-start | bytes 786436
  7.2 578.2 %all-gather.3.cloned.1.call-start = ((), (), s32[]{:S(2)}) async-start(), calls=%async_computation.4 | async-start | bytes 31457280 | tf_op jit(solution)/shard_map/all_gather | solution.py:74
  126.9 17.7 copy-start.7
  153.4 7.5 copy-start.11
  153.5 8.3 copy-start.4
  153.5 8.3 copy-start.10
  160.7 1454.9 %all-gather.5.cloned.1.call-start = ((), (), s32[]{:S(2)}) async-start(), calls=%async_computation.5 | async-start | bytes 31457280 | tf_op jit(solution)/shard_map/all_gather | solution.py:91
  585.4 17.0 copy-start.1
  945.6 21.5 %copy-start.2 = (f32[256,256]{1,0:T(8,128)S(1)}, f32[256,256]{1,0:T(8,128)}, u32[]{:S(2)}) copy-start(f32[256,256]{1,0:T(8,128)} %param.31) | copy-start | bytes 786436
  1013.4 19.9 %copy-start.9 = (f32[4,32,256]{2,1,0:T(8,128)S(1)}, f32[4,32,256]{2,1,0:T(8,128)}, u32[]{:S(2)}) copy-start(f32[4,32,256]{2,1,0:T(8,128)} %param.25) | copy-start | bytes 393220
  1024.7 8.5 copy-start.6
  1149.6 17.7 copy-start.8
  1645.6 28.8 %copy-start.12 = (f32[16,32]{1,0:T(8,128)S(1)}, f32[16,32]{1,0:T(8,128)}, u32[]{:S(2)}) copy-start(f32[16,32]{1,0:T(8,128)} %param.22) | copy-start | bytes 6148
  1674.5 17.3 copy-start.5
  1718.7 144.6 %all-to-all-start.3 = ((f32[384,32,256]{0,1,2:T(8,128)}), f32[384,32,256]{0,1,2:T(8,128)}, u32[]{:S(2)}, u32[]{:S(2)}) async-start(f32[384,32,256]{0,1,2:T(8,128)} %copy.68), calls=%async_computation.3 | async-start | bytes 25165824 | tf_op jit(solution)/shard_map/all_to_all | solution.py:31
  1879.4 12.9 copy-start.3
  1907.3 14.0 copy-start.13
  1907.3 26.4 %slice-start = ((s8[6291456]{0:T(1024)(128)(4,1)}), s8[2097152]{0:T(1024)(128)(4,1)S(1)}, s32[]{:S(2)}) async-start(s8[6291456]{0:T(1024)(128)(4,1)} %bitcast.112), calls=%async_computation.6 | async-start | bytes 4194304
  1921.3 12.4 slice-start.1
Sparse Core Ops, SparseCore 0:
  160.8 424.5 all-gather.2
  1194.1 421.4 all-gather.4
